TPU v7x, 128 devices: a whole 4x4x4 slice. The times are simulated.
128 devices in a mesh: row: 2 (over x_lo), col: 64 (over z, y, x_hi, core).
Axes of the slice: x: 4 (x_hi: 2, x_lo: 2; x = x_hi * 2 + x_lo), y: 4, z: 4, core: 2. Of those that a mesh axis runs over, the one named last changes fastest.
Arguments:
- panel: bfloat16 [196608, 1024], P('col', 'row'), may hold values from -0.1875 to 0.1875
- rhs: float32 [1024, 196608], P('row', 'col'), may hold values from -6 to 6
- diag_inverse: bfloat16 [2, 512, 512], replicated, may hold values from -1 to 2, as said below
Outputs:
- solved: bfloat16 [1024, 1024], P(None, 'row')
- updated: float32 [1024, 196608], P('row', 'col')
Inputs may be any that keep to these rules, and one draw needn't show every extreme that they name: `diag_inverse`: each block is lower triangular; its diagonal entries are 0.5 or more.
All inputs are finite; a program needn't handle non-finite values.
Results may differ from a plain program's by a relative error of at most 0.0065.
Values may be sent and summed in bfloat16 or wider, within the bound.
No kernel may reach another device: no remote copies, remote signals or barrier semaphores. Data moves between devices by JAX's collectives and lax.ppermute only.
A program may use at most 128 MiB of HBM per device.

v0:
```python
import jax
import jax.numpy as jnp
from jax import lax
from jax.sharding import PartitionSpec as P


def rows_for(lines, length):
    spare = -len(lines) % length
    return jnp.pad(lines, [(0, spare)] + [(0, 0)] * (lines.ndim - 1))


def broadcast_by_parts(value, axis, root):
    lines = jnp.where(lax.axis_index(axis) == root, value, jnp.zeros_like(value)).reshape(
        -1, *value.shape[1:][-1:]
    )
    padded = rows_for(lines, lax.axis_size(axis))
    own = lax.psum_scatter(padded, axis, scatter_dimension=0, tiled=True)
    return lax.all_gather(own, axis, axis=0, tiled=True)[: len(lines)].reshape(value.shape)


def from_everyone(value, axis):
    copies = jnp.broadcast_to(value, (lax.axis_size(axis), *value.shape))
    return lax.all_to_all(copies, axis, split_axis=0, concat_axis=0, tiled=True)


def taken_together(value, axis):
    return from_everyone(value, axis).sum(axis=0)


def split_up(value, dim, length):
    lengths = value.shape
    tiles = value.reshape(*lengths[:dim], length, lengths[dim] // length, *lengths[dim + 1 :])
    return jnp.moveaxis(tiles, dim, 0)


def sum_at_owner(value, axis, dim):
    tiles = split_up(value, dim, lax.axis_size(axis))
    arrived = lax.all_to_all(tiles, axis, split_axis=0, concat_axis=0, tiled=True)
    return arrived.astype(jnp.float32).sum(axis=0)


def spread_block(values, owner):
    return broadcast_by_parts(values, "col", owner)


def shards(panel, rhs, diag_inverse):
    block_size = diag_inverse.shape[1]
    step_count = diag_inverse.shape[0]
    rows_dev = panel.shape[0]
    slice_count = rhs.shape[0]
    rhs_count = slice_count * lax.axis_size("row")
    row_index = lax.axis_index("row")
    col_index = lax.axis_index("col")
    dropped = (col_index < step_count) & (row_index >= col_index)
    top_block = jnp.where(dropped, jnp.zeros_like(panel[:block_size]), panel[:block_size])
    masked = jnp.concatenate([top_block, panel[block_size:]], axis=0)
    contract = (((1,), (1,)), ((), ()))
    own_solved = jnp.zeros((rhs_count, block_size), jnp.bfloat16)
    products = jnp.zeros((rhs_count, rows_dev), jnp.float32)
    for current in range(step_count):
        inverse = diag_inverse[current].astype(jnp.float32)
        partial_value = lax.cond(
            col_index == current,
            lambda: lax.dot_general(
                own_solved, masked[:block_size], contract, preferred_element_type=jnp.float32
            ),
            lambda: jnp.zeros((rhs_count, block_size), jnp.float32),
        )
        embedded = lax.dynamic_update_slice(
            jnp.zeros((rhs_count, block_size), jnp.float32),
            rhs[:, :block_size],
            (row_index * slice_count, jnp.int32(0)),
        )
        residual = taken_together(embedded - partial_value, "row")
        whole_block = jnp.dot(residual, inverse.T, precision=lax.Precision.HIGHEST).astype(
            jnp.bfloat16
        )
        arrived = spread_block(whole_block, current)
        own_solved = jnp.where(row_index == current, arrived, own_solved)
        products = lax.cond(
            row_index == current,
            lambda: lax.dot_general(arrived, masked, contract, preferred_element_type=jnp.float32),
            lambda: products,
        )
    reduced = sum_at_owner(products.astype(jnp.bfloat16), "row", 0)
    updated = rhs - reduced
    return (own_solved, updated)


def solution(mesh):
    placed = (P("col", "row"), P("row", "col"), P())
    return jax.shard_map(
        shards,
        mesh=mesh,
        in_specs=placed,
        out_specs=(P(None, "row"), P("row", "col")),
        check_vma=False,
    )
```

profile of v0, /device:TPU:1, one launch (start us, length us, event | category | flops | bytes accessed | tf_op | source)
XLA Modules:
  0.0 1041.3 jit_solution(9920857579655382945)
XLA Ops:
  7.2 0.0 reduce-scatter.3.cloned.1.call-start
  7.2 1.1 slice_select_fusion
  8.3 0.2 broadcast.15
  8.6 1.3 slice_dynamic-update-slice_fusion
  9.9 1.6 conditional.4
  9.9 1.6 broadcast.10
  11.5 2.1 sub.9
  13.5 0.6 broadcast_in_dim.13
  14.1 50.4 %all_to_all.15 = f32[2,1024,512]{2,1,0:T(8,128)} all-to-all(f32[2,1024,512]{2,1,0:T(8,128)S(1)} %broadcast_in_dim.13), channel_id=1, replica_groups=mesh['row'=2,'col'=64] {'row'}, dimensions={0} | all-to-all | bytes 8388608 | tf_op jit(solution)/shard_map/all_to_all | solution.py:23
  64.6 4.2 reduce_sum.27
  68.7 4.5 fusion.3
  73.2 0.0 reduce-scatter.3.cloned.1.call-update
  73.2 0.0 all-gather.3.cloned.1.call-start
  73.3 334.0 %reduce-scatter.3.cloned.1.call-done = bf16[16,512]{1,0:T(8,128)(2,1)} async-done(((bf16[1024,512]{1,0:T(8,128)(2,1)}), bf16[16,512]{1,0:T(8,128)(2,1)}) %reduce-scatter.3.cloned.1.call-update) | async-done | bytes 16400 | tf_op jit(solution)/shard_map/reduce_scatter | solution.py:17
  407.3 0.0 all-gather.3.cloned.1.call-update
  407.3 0.0 reduce-scatter.5.cloned.1.call-start
  407.4 70.8 %all-gather.3.cloned.1.call-done = bf16[1024,512]{1,0:T(8,128)(2,1)} async-done(((bf16[16,512]{1,0:T(8,128)(2,1)}), bf16[1024,512]{1,0:T(8,128)(2,1)}) %all-gather.3.cloned.1.call-update) | async-done | bytes 1048592 | tf_op jit(solution)/shard_map/all_gather | solution.py:18
  478.1 2.3 broadcast_select_fusion
  480.4 3.3 conditional.5
  480.4 3.3 fusion.9
  483.7 2.1 sub.10
  485.8 0.6 broadcast_in_dim.14
  486.4 50.4 %all_to_all.16 = f32[2,1024,512]{2,1,0:T(8,128)} all-to-all(f32[2,1024,512]{2,1,0:T(8,128)S(1)} %broadcast_in_dim.14), channel_id=1, replica_groups=mesh['row'=2,'col'=64] {'row'}, dimensions={0} | all-to-all | bytes 8388608 | tf_op jit(solution)/shard_map/all_to_all | solution.py:23
  536.7 2.9 reduce_sum.28
  539.6 3.9 fusion.4
  543.4 0.0 slice-start
  543.4 0.0 reduce-scatter.5.cloned.1.call-update
  543.5 0.0 all-gather.5.cloned.1.call-start
  543.5 325.5 %reduce-scatter.5.cloned.1.call-done = bf16[16,512]{1,0:T(8,128)(2,1)} async-done(((bf16[1024,512]{1,0:T(8,128)(2,1)}), bf16[16,512]{1,0:T(8,128)(2,1)}) %reduce-scatter.5.cloned.1.call-update) | async-done | bytes 16400 | tf_op jit(solution)/shard_map/reduce_scatter | solution.py:17
  869.0 0.0 all-gather.5.cloned.1.call-update
  869.1 0.0 slice-done
  869.1 1.8 pad_maximum_fusion
  870.9 8.4 conditional.6
  870.9 8.4 fusion.10
  879.3 60.2 %all-gather.5.cloned.1.call-done = bf16[1024,512]{1,0:T(8,128)(2,1)} async-done(((bf16[16,512]{1,0:T(8,128)(2,1)}), bf16[1024,512]{1,0:T(8,128)(2,1)}) %all-gather.5.cloned.1.call-update) | async-done | bytes 1048592 | tf_op jit(solution)/shard_map/all_gather | solution.py:18
  939.5 0.0 copy-start
  939.5 0.0 copy-start.1
  939.5 10.1 all-to-all-start.2
  949.6 0.0 copy-done
  949.6 0.0 copy-done.1
  949.6 1.1 broadcast_select_fusion.1
  950.7 72.5 %all-to-all-done.2 = bf16[2,512,3072]{2,1,0:T(8,128)(2,1)} async-done(((bf16[2,512,3072]{2,1,0:T(8,128)(2,1)}), bf16[2,512,3072]{2,1,0:T(8,128)(2,1)}, u32[]{:S(2)}, u32[]{:S(2)}) %all-to-all-start.2) | async-done | bytes 6291488 | tf_op jit(solution)/shard_map/all_to_all | solution.py:38
  1023.1 5.0 convert_reduce_fusion
  1028.1 6.6 sub.11
  (1 shorter events, 0.0 us)
Async XLA Ops:
  7.2 400.1 %reduce-scatter.3.cloned.1.call-start = ((), (), s32[]{:S(2)}) async-start(), calls=%async_computation.5 | async-start | bytes 1064960 | tf_op jit(solution)/shard_map/reduce_scatter | solution.py:17
  73.2 404.9 %all-gather.3.cloned.1.call-start = ((), (), s32[]{:S(2)}) async-start(), calls=%async_computation.6 | async-start | bytes 1064960 | tf_op jit(solution)/shard_map/all_gather | solution.py:18
  407.3 461.7 %reduce-scatter.5.cloned.1.call-start = ((), (), s32[]{:S(2)}) async-start(), calls=%async_computation.7 | async-start | bytes 1064960 | tf_op jit(solution)/shard_map/reduce_scatter | solution.py:17
  543.4 325.6 %slice-start = ((bf16[3072,512]{1,0:T(8,128)(2,1)}), bf16[2560,512]{1,0:T(8,128)(2,1)S(1)}, s32[]{:S(2)}) async-start(bf16[3072,512]{1,0:T(8,128)(2,1)} %param.11), calls=%async_computation.9 | async-start | bytes 5242880 | tf_op jit(solution)/shard_map/slice | solution.py:56
  543.5 396.0 %all-gather.5.cloned.1.call-start = ((), (), s32[]{:S(2)}) async-start(), calls=%async_computation.8 | async-start | bytes 1064960 | tf_op jit(solution)/shard_map/all_gather | solution.py:18
  939.5 10.1 copy-start
  939.5 10.1 copy-start.1
  939.5 83.6 %all-to-all-start.2 = ((bf16[2,512,3072]{2,1,0:T(8,128)(2,1)}), bf16[2,512,3072]{2,1,0:T(8,128)(2,1)}, u32[]{:S(2)}, u32[]{:S(2)}) async-start(bf16[2,512,3072]{2,1,0:T(8,128)(2,1)} %bitcast.16), calls=%async_computation.4 | async-start | bytes 12582912 | tf_op jit(solution)/shard_map/all_to_all | solution.py:38
Sparse Core Ops, SparseCore 0:
  73.3 333.9 reduce-scatter.2
  410.5 67.5 all-gather.2
  543.6 325.4 reduce-scatter.4
  872.1 67.3 all-gather.4
where the time goes:
time: 1040 us
  waiting for transfers between devices  863 us (83%)
  blocking collectives  101 us (10%)
  other arithmetic  29 us (3%)
  matrix products  20 us (2%)
  between operations  13.8 us (1%)
    reduce_scatter x2, waiting for transfers between devices, broadcast_by_parts(): own = lax.psum_scatter(padded, axis, scatter_dimension=0, tiled=True)  660 us
    all_gather x2, waiting for transfers between devices, broadcast_by_parts(): lax.all_gather(own, axis, axis=0, tiled=True)[:len(lines)]  131 us
    all_to_all x2, blocking collectives, from_everyone(): return lax.all_to_all(copies, axis, split_axis=0, concat_axis=0, tiled=True)  101 us
    all_to_all x1, waiting for transfers between devices, sum_at_owner(): lax.all_to_all(tiles, axis, split_axis=0, concat_axis=0, tiled=True)  72.5 us
  transfers between devices with their start and end apart: 5, of which 5 were waited for; matrix products, arithmetic and copies ran while one was open for 1% of the time, Pallas kernels for 0%

commit v1 on v0

--- a/solution.py
+++ b/solution.py
@@ -2,6 +2,11 @@
 import jax.numpy as jnp
 from jax import lax
 from jax.sharding import PartitionSpec as P
+
+
+def gather_over(block, name, along):
+    repeated = jnp.stack([block] * lax.axis_size(name))
+    return jnp.concatenate(lax.all_to_all(repeated, name, 0, 0), axis=along)
 
 
 def rows_for(lines, length):
@@ -15,7 +20,7 @@
     )
     padded = rows_for(lines, lax.axis_size(axis))
     own = lax.psum_scatter(padded, axis, scatter_dimension=0, tiled=True)
-    return lax.all_gather(own, axis, axis=0, tiled=True)[: len(lines)].reshape(value.shape)
+    return gather_over(own, axis, 0)[: len(lines)].reshape(value.shape)
 
 
 def from_everyone(value, axis):

time: 1040 us -> 967 us (0.930)
  waiting for transfers between devices: 863 us -> 757 us
  starting transfers between devices: 10.2 us -> 35.1 us
    all_gather x2 -> x0, waiting for transfers between devices: 131 us -> none  [broadcast_by_parts(): lax.all_gather(own, axis, axis=0, tiled=True)[:len(lines)]]
    all_to_all x0 -> x2, waiting for transfers between devices: none -> 27.6 us  [gather_over(): return jnp.concatenate(lax.all_to_all(repeated, name, 0, 0), axis=along)]
    all_to_all x0 -> x2, starting transfers between devices: none -> 24.9 us  [gather_over(): return jnp.concatenate(lax.all_to_all(repeated, name, 0, 0), axis=along)]
where the time goes in v1:
time: 967 us; the launch traced here: 966 us
  waiting for transfers between devices  757 us (78%)
  blocking collectives  101 us (10%)
  starting transfers between devices  35.1 us (4%)
  other arithmetic  29.3 us (3%)
  matrix products  19 us (2%)
  between operations  14.2 us (1%)
  local copies, waits for them, and re-layouts  9.94 us (1%)
    reduce_scatter x2, waiting for transfers between devices, broadcast_by_parts(): own = lax.psum_scatter(padded, axis, scatter_dimension=0, tiled=True)  659 us
    all_to_all x2, blocking collectives, from_everyone(): return lax.all_to_all(copies, axis, split_axis=0, concat_axis=0, tiled=True)  101 us
    all_to_all x1, waiting for transfers between devices, sum_at_owner(): lax.all_to_all(tiles, axis, split_axis=0, concat_axis=0, tiled=True)  71 us
    all_to_all x2, waiting for transfers between devices, gather_over(): return jnp.concatenate(lax.all_to_all(repeated, name, 0, 0), axis=along)  27.6 us
    all_to_all x2, starting transfers between devices, gather_over(): return jnp.concatenate(lax.all_to_all(repeated, name, 0, 0), axis=along)  24.9 us
  transfers between devices with their start and end apart: 5, of which 5 were waited for; matrix products, arithmetic and copies ran while one was open for 1% of the time, Pallas kernels for 0%

profile of v1, /device:TPU:1, one launch (start us, length us, event | category | flops | bytes accessed | tf_op | source)
XLA Modules:
  0.0 965.8 jit_solution(3629831655837502180)
XLA Ops:
  7.2 0.0 reduce-scatter.3.cloned.1.call-start
  7.2 1.1 slice_select_fusion
  8.3 0.0 copy-start.2
  8.3 0.2 broadcast.19
  8.6 1.3 slice_dynamic-update-slice_fusion
  9.9 0.0 copy-done.2
  9.9 1.6 conditional.4
  9.9 1.6 broadcast.14
  11.5 2.1 sub.9
  13.6 0.6 broadcast_in_dim.13
  14.2 50.4 %all_to_all.25 = f32[2,1024,512]{2,1,0:T(8,128)} all-to-all(f32[2,1024,512]{2,1,0:T(8,128)S(1)} %broadcast_in_dim.13), channel_id=1, replica_groups=mesh['row'=2,'col'=64] {'row'}, dimensions={0} | all-to-all | bytes 8388608 | tf_op jit(solution)/shard_map/all_to_all | solution.py:28
  64.6 4.2 reduce_sum.27
  68.8 0.0 copy-done.4
  68.8 4.4 fusion.3
  73.2 0.0 reduce-scatter.3.cloned.1.call-update
  73.2 334.2 %reduce-scatter.3.cloned.1.call-done = bf16[16,512]{1,0:T(8,128)(2,1)} async-done(((bf16[1024,512]{1,0:T(8,128)(2,1)}), bf16[16,512]{1,0:T(8,128)(2,1)}) %reduce-scatter.3.cloned.1.call-update) | async-done | bytes 16400 | tf_op jit(solution)/shard_map/reduce_scatter | solution.py:22
  407.5 1.8 stack.4
  409.3 12.1 %all-to-all-start.1 = ((bf16[64,16,512]{2,1,0:T(8,128)(2,1)}), bf16[64,16,512]{2,1,0:T(8,128)(2,1)S(1)}, u32[]{:S(2)}, u32[]{:S(2)}) async-start(bf16[64,16,512]{2,1,0:T(8,128)(2,1)} %stack.4), calls=%async_computation.2 | async-start | bytes 2097152 | tf_op jit(solution)/shard_map/all_to_all | solution.py:9
  421.4 0.0 reduce-scatter.5.cloned.1.call-start
  421.4 19.9 %all-to-all-done.1 = bf16[64,16,512]{2,1,0:T(8,128)(2,1)S(1)} async-done(((bf16[64,16,512]{2,1,0:T(8,128)(2,1)}), bf16[64,16,512]{2,1,0:T(8,128)(2,1)S(1)}, u32[]{:S(2)}, u32[]{:S(2)}) %all-to-all-start.1) | async-done | bytes 1048608 | tf_op jit(solution)/shard_map/all_to_all | solution.py:9
  441.3 1.2 broadcast_select_fusion
  442.5 0.2 copy-done
  442.7 3.4 conditional.5
  442.7 3.4 fusion.9
  446.1 2.1 sub.10
  448.2 0.6 broadcast_in_dim.14
  448.8 50.5 %all_to_all.26 = f32[2,1024,512]{2,1,0:T(8,128)} all-to-all(f32[2,1024,512]{2,1,0:T(8,128)S(1)} %broadcast_in_dim.14), channel_id=1, replica_groups=mesh['row'=2,'col'=64] {'row'}, dimensions={0} | all-to-all | bytes 8388608 | tf_op jit(solution)/shard_map/all_to_all | solution.py:28
  499.3 2.9 reduce_sum.28
  502.2 0.0 copy-done.5
  502.2 2.8 fusion.4
  505.0 0.0 reduce-scatter.5.cloned.1.call-update
  505.0 324.5 %reduce-scatter.5.cloned.1.call-done = bf16[16,512]{1,0:T(8,128)(2,1)} async-done(((bf16[1024,512]{1,0:T(8,128)(2,1)}), bf16[16,512]{1,0:T(8,128)(2,1)}) %reduce-scatter.5.cloned.1.call-update) | async-done | bytes 16400 | tf_op jit(solution)/shard_map/reduce_scatter | solution.py:22
  829.5 1.8 stack.5
  831.3 12.8 %all-to-all-start.3 = ((bf16[64,16,512]{2,1,0:T(8,128)(2,1)}), bf16[64,16,512]{2,1,0:T(8,128)(2,1)}, u32[]{:S(2)}, u32[]{:S(2)}) async-start(bf16[64,16,512]{2,1,0:T(8,128)(2,1)} %stack.5), calls=%async_computation.5 | async-start | bytes 2097152 | tf_op jit(solution)/shard_map/all_to_all | solution.py:9
  844.2 0.0 slice-start
  844.2 0.0 copy-start.3
  844.2 1.7 slice-done
  845.9 0.1 copy-done.3
  846.0 1.8 pad_maximum_fusion
  847.8 8.4 conditional.6
  847.8 8.4 fusion.10
  856.2 7.8 all-to-all-done.3
  864.0 10.1 %all-to-all-start.4 = ((bf16[2,512,3072]{2,1,0:T(8,128)(2,1)}), bf16[2,512,3072]{2,1,0:T(8,128)(2,1)}, u32[]{:S(2)}, u32[]{:S(2)}) async-start(bf16[2,512,3072]{2,1,0:T(8,128)(2,1)} %bitcast.22), calls=%async_computation.6 | async-start | bytes 12582912 | tf_op jit(solution)/shard_map/all_to_all | solution.py:43
  874.1 0.0 copy-done.1
  874.1 2.3 broadcast_select_fusion.1
  876.4 71.0 %all-to-all-done.4 = bf16[2,512,3072]{2,1,0:T(8,128)(2,1)} async-done(((bf16[2,512,3072]{2,1,0:T(8,128)(2,1)}), bf16[2,512,3072]{2,1,0:T(8,128)(2,1)}, u32[]{:S(2)}, u32[]{:S(2)}) %all-to-all-start.4) | async-done | bytes 6291488 | tf_op jit(solution)/shard_map/all_to_all | solution.py:43
  947.4 5.0 convert_reduce_fusion
  952.4 6.6 sub.11
  (5 shorter events, 0.0 us)
Async XLA Ops:
  7.2 400.3 %reduce-scatter.3.cloned.1.call-start = ((), (), s32[]{:S(2)}) async-start(), calls=%async_computation.7 | async-start | bytes 1064960 | tf_op jit(solution)/shard_map/reduce_scatter | solution.py:22
  8.3 1.6 copy-start.2
  64.6 4.2 copy-start.4
  409.3 32.0 %all-to-all-start.1 = ((bf16[64,16,512]{2,1,0:T(8,128)(2,1)}), bf16[64,16,512]{2,1,0:T(8,128)(2,1)S(1)}, u32[]{:S(2)}, u32[]{:S(2)}) async-start(bf16[64,16,512]{2,1,0:T(8,128)(2,1)} %stack.4), calls=%async_computation.2 | async-start | bytes 2097152 | tf_op jit(solution)/shard_map/all_to_all | solution.py:9
  421.4 408.1 %reduce-scatter.5.cloned.1.call-start = ((), (), s32[]{:S(2)}) async-start(), calls=%async_computation.8 | async-start | bytes 1064960 | tf_op jit(solution)/shard_map/reduce_scatter | solution.py:22
  441.3 1.4 copy-start
  499.3 2.9 copy-start.5
  831.3 32.7 %all-to-all-start.3 = ((bf16[64,16,512]{2,1,0:T(8,128)(2,1)}), bf16[64,16,512]{2,1,0:T(8,128)(2,1)}, u32[]{:S(2)}, u32[]{:S(2)}) async-start(bf16[64,16,512]{2,1,0:T(8,128)(2,1)} %stack.5), calls=%async_computation.5 | async-start | bytes 2097152 | tf_op jit(solution)/shard_map/all_to_all | solution.py:9
  844.2 1.7 slice-start
  844.2 1.8 copy-start.3
  864.0 10.1 %copy-start.1 = (bf16[64,16,512]{2,1,0:T(8,128)(2,1)S(1)}, bf16[64,16,512]{2,1,0:T(8,128)(2,1)}, u32[]{:S(2)}) copy-start(bf16[64,16,512]{2,1,0:T(8,128)(2,1)} %copy-done) | copy-start | bytes 3145732
  864.0 83.4 %all-to-all-start.4 = ((bf16[2,512,3072]{2,1,0:T(8,128)(2,1)}), bf16[2,512,3072]{2,1,0:T(8,128)(2,1)}, u32[]{:S(2)}, u32[]{:S(2)}) async-start(bf16[2,512,3072]{2,1,0:T(8,128)(2,1)} %bitcast.22), calls=%async_computation.6 | async-start | bytes 12582912 | tf_op jit(solution)/shard_map/all_to_all | solution.py:43
Sparse Core Ops, SparseCore 0:
  73.3 334.0 reduce-scatter.2
  505.1 324.3 reduce-scatter.4
